TPU v7x, 32 devices: a whole 2x2x4 slice. The times are simulated.
32 devices in a mesh: dp: 2 (over core), tvoc: 4 (over y, x), svoc: 4 (over z).
Axes of the slice: x: 2, y: 2, z: 4, core: 2. Of those that a mesh axis runs over, the one named last changes fastest.
Arguments:
- teacher_probs: bfloat16 [256, 20480], P('dp', 'tvoc'), may hold values from 0 to 1, as said below
- block_values: bfloat16 [4, 4, 24, 128, 128], P('tvoc', 'svoc'), may hold values from 0.0099487305 to 1
- block_index: int32 [4, 4, 24, 2], P('tvoc', 'svoc'), may hold values from 0 to 39, as said below
- block_count: int32 [4, 4], P('tvoc', 'svoc'), may hold values from 5 to 24, as said below
- hidden: bfloat16 [256, 3072], P('dp'), may hold values from -48 to 48
- student_weight: bfloat16 [3072, 8192], P(None, ('tvoc', 'svoc')), may hold values from -0.15 to 0.15
Outputs:
- divergence: float32 [256], P('dp')
- grad_weight: bfloat16 [3072, 8192], P('dp', ('tvoc', 'svoc'))
- grad_hidden: float32 [256, 3072], P('dp', ('tvoc', 'svoc'))
Inputs may be any that keep to these rules, and one draw needn't show every extreme that they name: `teacher_probs`: each row sums to one and every entry is positive. `block_index`: The live slots of one device name at most 2 distinct c with the same c // 4, and some value of c // 4 reaches 2 on every device. Several live slots may name the same c, with the same or another teacher block. `block_count`: the live slots are the first ones; some device has all 24 live.
All inputs are finite; a program needn't handle non-finite values.
Results may differ from a plain program's by a relative error of at most 0.013.
Values may be sent and summed in bfloat16 or wider, within the bound.
A program may use at most 64 MiB of HBM per device.

v0:
```python
import functools

import jax
import jax.numpy as jnp
from jax import lax
from jax.experimental import pallas as pl
from jax.experimental.pallas import tpu as pltpu
from jax.sharding import PartitionSpec as P

loss_scale = 128.0
cap = 2
tag_rows = 16
MESH = pl.DeviceIdType.MESH
f32, bf16 = jnp.float32, jnp.bfloat16


def kernel(
    n_t, n_s, blk,
    idx_s, cnt_s, teacher_hbm, values_hbm, hidden_hbm, weight_hbm,
    div_ref, gw_ref, gh_ref,
    teacher, values, hidden, weight, peer_hidden, hid_t, mapped, targets, tags,
    packed, landed, mass, logits, shifted, stats, grads, grad_t, gh_t, own_t, out1, in1, out2, in2,
    block_sem, load_sem, ph_sem, pk_send, pk_recv, st_send, st_recv, lg_sem, s1, r1, s2, r2,
):
    d, i, j = lax.axis_index("dp"), lax.axis_index("tvoc"), lax.axis_index("svoc")
    n_d = 2
    n = n_t * n_s
    me = i * n_s + j
    other = n_d - 1 - d
    tokens, width = hidden.shape
    shard = weight.shape[1]
    per_owner = shard // blk
    half = width // n_d
    rows = width // n

    slots, blocks = values.shape[0], teacher.shape[0]
    loads = [
        pltpu.make_async_copy(src, dst, load_sem.at[k])
        for k, (src, dst) in enumerate(((values_hbm.at[0, 0], values), (hidden_hbm, hidden), (weight_hbm, weight)))
    ]
    loads[0].start()

    def block_load(b):
        return pltpu.make_async_copy(
            teacher_hbm.at[:, pl.ds(pl.multiple_of(b * blk, blk), blk)], teacher.at[b], block_sem.at[b])

    def block_start(b, carry):
        block_load(b).start()
        return carry

    lax.fori_loop(0, blocks, block_start, 0)
    loads[1].start()
    loads[2].start()

    def peer(q):
        r = lax.rem(me + q, n)
        return r, {"tvoc": r // n_s, "svoc": lax.rem(r, n_s)}

    barrier = pltpu.get_barrier_semaphore()

    def greet(q, carry):
        pl.semaphore_signal(barrier, inc=1, device_id=peer(q)[1], device_id_type=MESH)
        return carry

    lax.fori_loop(1, n, greet, 0)
    pl.semaphore_signal(barrier, inc=1, device_id={"dp": other}, device_id_type=MESH)

    lanes = targets.shape[1]
    lane = lax.broadcasted_iota(jnp.int32, (slots, lanes), 1)
    slot = lax.broadcasted_iota(jnp.int32, (slots, lanes), 0)
    column = jnp.zeros((slots, lanes), jnp.int32)
    for s in range(slots):
        column = jnp.where(slot == s, idx_s[0, 0, 1, s], column)
    hot = (column == lane) & (slot < cnt_s[0, 0])
    present = jnp.max(jnp.where(hot, 1.0, 0.0), axis=0, keepdims=True)
    r_iota = lax.broadcasted_iota(jnp.int32, (lanes, lanes), 0).astype(f32)
    c_iota = lax.broadcasted_iota(jnp.int32, (lanes, lanes), 1).astype(f32)
    r_own = jnp.floor((r_iota + 0.5) / per_owner)
    c_own = jnp.floor((c_iota + 0.5) / per_owner)
    below = jnp.where((r_own == c_own) & (r_iota < c_iota), 1.0, 0.0)
    rank = jnp.dot(jnp.broadcast_to(present, (8, lanes)), below, preferred_element_type=f32)[0:1]
    place = cap * c_own[0:1] + rank
    goal = jnp.sum(jnp.where(hot, place + 1.0, 0.0), axis=1, keepdims=True) - 1.0
    targets[...] = jnp.broadcast_to(goal, (slots, lanes))
    n_tags = tags.shape[0]
    t_iota = lax.broadcasted_iota(jnp.int32, (n_tags, lanes), 0).astype(f32)
    within = c_iota[0:1] - per_owner * c_own[0:1]
    tag = jnp.sum(jnp.where((present > 0.0) & (place == t_iota), within + 1.0, 0.0), axis=1, keepdims=True) - 1.0
    tags[...] = jnp.broadcast_to(tag, (n_tags, lanes))

    def block_wait(b, carry):
        block_load(b).wait()
        return carry

    loads[0].wait()
    lax.fori_loop(0, blocks, block_wait, 0)
    for s in range(slots):
        mapped[s] = jnp.dot(teacher[idx_s[0, 0, 0, s]], values[s], preferred_element_type=f32)

    def pack(q, carry):
        o = lax.rem(i + q, n_t)
        for k in range(cap):
            t = (o * cap + k).astype(f32)
            acc = jnp.zeros((tokens, blk), f32)
            for s in range(slots):
                acc = acc + jnp.where(targets[s:s + 1, 0:blk] == t, mapped[s], 0.0)
            packed[o, 0:tokens, k * blk:(k + 1) * blk] = acc.astype(bf16)
            packed[o, tokens:tokens + tag_rows, k * blk:(k + 1) * blk] = jnp.broadcast_to(
                tags[pl.ds(o * cap + k, 1), 0:blk], (tag_rows, blk)).astype(bf16)
        return carry

    lax.fori_loop(1, n_t, pack, 0)

    pl.semaphore_wait(barrier, n)

    def hidden_copy():
        start = pl.multiple_of(other * half, blk)
        return pltpu.make_async_remote_copy(
            src_ref=hidden.at[:, pl.ds(start, half)], dst_ref=peer_hidden,
            send_sem=ph_sem.at[0], recv_sem=ph_sem.at[1],
            device_id={"dp": other}, device_id_type=MESH)

    def packed_copy(o, src):
        return pltpu.make_async_remote_copy(
            src_ref=packed.at[o], dst_ref=landed.at[src],
            send_sem=pk_send.at[o], recv_sem=pk_recv.at[src],
            device_id={"tvoc": o}, device_id_type=MESH)

    def pack_send(q, carry):
        o = lax.rem(i + q, n_t)
        packed_copy(o, i).start()
        return carry

    lax.fori_loop(1, n_t, pack_send, 0)
    loads[1].wait()
    hidden_copy().start()
    pack(0, 0)

    loads[2].wait()
    depth = 4 * blk
    logits[...] = jnp.zeros_like(logits)

    def logit_step(k, carry):
        at = pl.multiple_of(k * depth, depth)
        logits[...] += jnp.dot(hidden[:, pl.ds(at, depth)], weight[pl.ds(at, depth), :], preferred_element_type=f32)
        return carry

    lax.fori_loop(0, width // depth, logit_step, 0)

    lg = logits[...]
    top = jnp.max(lg, axis=1, keepdims=True)
    e = jnp.exp(lg - top)
    e_sum = jnp.sum(e, axis=1, keepdims=True)
    shifted[...] = e


    own_at = d * half

    def turn_own(k, carry):
        at = pl.multiple_of(k * blk, blk)
        tile = hidden[:, pl.ds(pl.multiple_of(own_at + at, blk), blk)].astype(f32)
        hid_t[pl.ds(at, blk), 0:tokens] = tile.T.astype(bf16)
        return carry

    lax.fori_loop(0, half // blk, turn_own, 0)

    def add_mass(ref, o, first):
        for b in range(per_owner):
            acc = jnp.zeros((tokens, blk), f32) if first else mass[:, b * blk:(b + 1) * blk]
            for k in range(cap):
                which = ref[o, tokens:tokens + 1, k * blk:(k + 1) * blk].astype(f32)
                part = ref[o, 0:tokens, k * blk:(k + 1) * blk].astype(f32)
                acc = acc + jnp.where(which == float(b), part, 0.0)
            mass[:, b * blk:(b + 1) * blk] = acc

    add_mass(packed, i, True)

    def take_mass(q, carry):
        o = lax.rem(i + q, n_t)
        packed_copy(o, o).wait_recv()
        add_mass(landed, o, False)
        return carry

    lax.fori_loop(1, n_t, take_mass, 0)

    lg = logits[...]
    tm = mass[...]
    positive = tm > 0
    parts = (
        top,
        e_sum,
        jnp.sum(tm, axis=1, keepdims=True),
        jnp.sum(jnp.where(positive, tm * jnp.log(jnp.where(positive, tm, 1.0)), 0.0), axis=1, keepdims=True),
        jnp.sum(tm * lg, axis=1, keepdims=True),
    )
    spot = lax.broadcasted_iota(jnp.int32, (tokens, 128), 1)
    wide = jnp.zeros((tokens, 128), f32)
    for k, part in enumerate(parts):
        wide = jnp.where(spot == k, part, wide)
    stats[me] = wide.T[0:8]

    def stat_copy(q, src):
        r, where = peer(q)
        return pltpu.make_async_remote_copy(
            src_ref=stats.at[me], dst_ref=stats.at[src],
            send_sem=st_send.at[q], recv_sem=st_recv.at[src],
            device_id=where, device_id_type=MESH)

    def stat_send(q, carry):
        stat_copy(q, me).start()
        return carry

    lax.fori_loop(1, n, stat_send, 0)

    hidden_copy().wait_recv()

    def turn_peer(k, carry):
        at = pl.multiple_of(k * blk, blk)
        hid_t[pl.ds(at, blk), tokens:2 * tokens] = peer_hidden[:, pl.ds(at, blk)].astype(f32).T.astype(bf16)
        return carry

    lax.fori_loop(0, half // blk, turn_peer, 0)

    def stat_wait(q, carry):
        stat_copy(q, peer(q)[0]).wait_recv()
        return carry

    lax.fori_loop(1, n, stat_wait, 0)
    st = stats[...]
    largest = jnp.max(st, axis=0)[0:1]
    scale = jnp.exp(st[:, 0:1, :] - largest[None])
    line = lax.broadcasted_iota(jnp.int32, st.shape, 1)
    sums = jnp.sum(jnp.where(line == 1, st * scale, st), axis=0)
    total, mass_sum, entropy, cross = sums[1:2], sums[2:3], sums[3:4], sums[4:5]
    div_ref[...] = entropy / mass_sum - jnp.log(mass_sum) - cross / mass_sum + largest + jnp.log(total)
    rows8 = lax.broadcasted_iota(jnp.int32, (128, tokens), 0)
    back = jnp.where(rows8 == 0, largest, jnp.where(rows8 == 1, loss_scale / total, loss_scale / mass_sum)).T
    factor = jnp.exp(top - back[:, 0:1]) * back[:, 1:2]
    g = shifted[...] * factor - mass[...] * back[:, 2:3]
    grads[0:tokens, :] = g.astype(bf16)
    lg_copy = pltpu.make_async_remote_copy(
        src_ref=grads.at[pl.ds(0, tokens)], dst_ref=grads.at[pl.ds(tokens, tokens)],
        send_sem=lg_sem.at[0], recv_sem=lg_sem.at[1],
        device_id={"dp": other}, device_id_type=MESH)
    lg_copy.start()
    grad_t[...] = g.T.astype(bf16)

    direct = rows % 16 == 0
    if not direct:
        tile = 2 * blk

        def gh_step(k, carry):
            at = pl.multiple_of(k * tile, tile)
            gh_t[pl.ds(at, tile), :] = jnp.dot(weight[pl.ds(at, tile), :], grad_t[...], preferred_element_type=f32)
            return carry

        lax.fori_loop(0, width // tile, gh_step, 0)

    def chunk(ii, jj):
        start = (ii * n_s + jj) * rows
        if not direct:
            return gh_t[pl.ds(pl.multiple_of(start, 8), rows), :]
        return jnp.dot(weight[pl.ds(pl.multiple_of(start, 16), rows), :], grad_t[...], preferred_element_type=f32)

    def copy1(ii, jj, src):
        return pltpu.make_async_remote_copy(
            src_ref=out1.at[ii, jj], dst_ref=in1.at[src, jj],
            send_sem=s1.at[ii, jj], recv_sem=r1.at[src, jj],
            device_id={"tvoc": ii}, device_id_type=MESH)

    def copy2(jj, src):
        return pltpu.make_async_remote_copy(
            src_ref=out2.at[jj], dst_ref=in2.at[src],
            send_sem=s2.at[jj], recv_sem=r2.at[src],
            device_id={"svoc": jj}, device_id_type=MESH)

    def send1(p, carry):
        jj = lax.rem(j + p, n_s)

        def inner(q, c):
            ii = lax.rem(i + q, n_t)
            out1[ii, jj] = chunk(ii, jj).astype(bf16)
            copy1(ii, jj, i).start()
            return c

        return lax.fori_loop(1, n_t, inner, carry)

    lax.fori_loop(1, n_s + 1, send1, 0)

    def own_chunk(p, carry):
        jj = lax.rem(j + p, n_s)
        own_t[jj] = chunk(i, jj)
        return carry

    lax.fori_loop(1, n_s + 1, own_chunk, 0)

    lg_copy.wait_recv()

    tall = 2 * blk

    def gw_step(k, carry):
        at = pl.multiple_of(k * tall, tall)
        gw_ref[pl.ds(at, tall), :] = jnp.dot(
            hid_t[pl.ds(at, tall), :], grads[...], preferred_element_type=f32).astype(bf16)
        return carry

    lax.fori_loop(0, half // tall, gw_step, 0)

    def gather1(jj):
        acc = own_t[jj]
        for q in range(1, n_t):
            ii = lax.rem(i + q, n_t)
            copy1(ii, jj, ii).wait_recv()
            acc = acc + in1[ii, jj].astype(f32)
        return acc

    def send2(p, carry):
        jj = lax.rem(j + p, n_s)
        out2[jj] = gather1(jj).astype(bf16)
        copy2(jj, j).start()
        return carry

    lax.fori_loop(1, n_s, send2, 0)
    acc = gather1(j)
    for p in range(1, n_s):
        jj = lax.rem(j + p, n_s)
        copy2(jj, jj).wait_recv()
        acc = acc + in2[jj].astype(f32)
    gh_ref[...] = acc

    hidden_copy().wait_send()
    lg_copy.wait_send()

    def drain_packed(q, carry):
        o = lax.rem(i + q, n_t)
        packed_copy(o, i).wait_send()
        return carry

    lax.fori_loop(1, n_t, drain_packed, 0)

    def drain_stats(q, carry):
        stat_copy(q, me).wait_send()
        return carry

    lax.fori_loop(1, n, drain_stats, 0)

    def drain1(p, carry):
        jj = lax.rem(j + p, n_s)

        def inner(q, c):
            copy1(lax.rem(i + q, n_t), jj, i).wait_send()
            return c

        return lax.fori_loop(1, n_t, inner, carry)

    lax.fori_loop(1, n_s + 1, drain1, 0)

    def drain2(p, carry):
        copy2(lax.rem(j + p, n_s), j).wait_send()
        return carry

    lax.fori_loop(1, n_s, drain2, 0)


def flush(div, gw, gh, div_out, gw_out, gh_out, sem):
    copies = [
        pltpu.make_async_copy(src, dst, sem.at[k])
        for k, (src, dst) in enumerate(((gw, gw_out), (gh, gh_out), (div, div_out)))
    ]
    for copy in copies:
        copy.start()
    for copy in copies:
        copy.wait()


def local(n_t, n_s, teacher_probs, block_values, block_index, block_count, hidden, student_weight):
    tokens, width = hidden.shape
    slots, blk = block_values.shape[2], block_values.shape[3]
    shard = student_weight.shape[1]
    half, rows, n = width // 2, width // (n_t * n_s), n_t * n_s
    lanes = -(-(n_t * (shard // blk)) // 128) * 128
    vmem, smem = pl.BlockSpec(memory_space=pltpu.VMEM), pl.BlockSpec(memory_space=pltpu.SMEM)
    hbm = pl.BlockSpec(memory_space=pltpu.HBM)
    DMA = pltpu.SemaphoreType.DMA
    parcel = (n_t, tokens + tag_rows, cap * blk)
    div, gw, gh = pl.pallas_call(
        functools.partial(kernel, n_t, n_s, blk),
        out_shape=(
            jax.ShapeDtypeStruct((1, tokens), f32),
            jax.ShapeDtypeStruct((half, shard), bf16),
            jax.ShapeDtypeStruct((rows, tokens), f32),
        ),
        in_specs=[smem, smem, hbm, hbm, hbm, hbm],
        out_specs=(vmem, vmem, vmem),
        scratch_shapes=[
            pltpu.VMEM((teacher_probs.shape[1] // blk, tokens, blk), bf16),
            pltpu.VMEM(block_values.shape[2:], bf16),
            pltpu.VMEM(hidden.shape, bf16),
            pltpu.VMEM(student_weight.shape, bf16),
            pltpu.VMEM((tokens, half), bf16),
            pltpu.VMEM((half, 2 * tokens), bf16),
            pltpu.VMEM((slots, tokens, blk), f32),
            pltpu.VMEM((slots, lanes), f32),
            pltpu.VMEM((n_t * cap, lanes), f32),
            pltpu.VMEM(parcel, bf16),
            pltpu.VMEM(parcel, bf16),
            pltpu.VMEM((tokens, shard), f32),
            pltpu.VMEM((tokens, shard), f32),
            pltpu.VMEM((tokens, shard), f32),
            pltpu.VMEM((n, 8, tokens), f32),
            pltpu.VMEM((2 * tokens, shard), bf16),
            pltpu.VMEM((shard, tokens), bf16),
            pltpu.VMEM((width, tokens), f32),
            pltpu.VMEM((n_s, rows, tokens), f32),
            pltpu.VMEM((n_t, n_s, rows, tokens), bf16),
            pltpu.VMEM((n_t, n_s, rows, tokens), bf16),
            pltpu.VMEM((n_s, rows, tokens), bf16),
            pltpu.VMEM((n_s, rows, tokens), bf16),
            DMA((teacher_probs.shape[1] // blk,)), DMA((3,)), DMA((2,)), DMA((n_t,)), DMA((n_t,)), DMA((n,)), DMA((n,)), DMA((2,)),
            DMA((n_t, n_s)), DMA((n_t, n_s)), DMA((n_s,)), DMA((n_s,)),
        ],
        compiler_params=pltpu.CompilerParams(
            collective_id=0, has_side_effects=True, vmem_limit_bytes=32 * 1024 * 1024),
    )(
        pltpu.with_memory_space_constraint(jnp.swapaxes(block_index, 2, 3), pltpu.HBM), block_count,
        *(pltpu.with_memory_space_constraint(x, pltpu.HBM) for x in (teacher_probs, block_values, hidden, student_weight)))
    div, gw, gh = pl.pallas_call(
        flush,
        out_shape=tuple(jax.ShapeDtypeStruct(x.shape, x.dtype) for x in (div, gw, gh)),
        in_specs=[vmem] * 3,
        out_specs=(hbm,) * 3,
        scratch_shapes=[DMA((3,))],
        compiler_params=pltpu.CompilerParams(vmem_limit_bytes=2**20),
    )(div, gw, gh)
    return div.reshape(tokens), gw, gh.T


def solution(mesh):
    return jax.shard_map(
        functools.partial(local, mesh.shape["tvoc"], mesh.shape["svoc"]),
        mesh=mesh,
        in_specs=(
            P("dp", "tvoc"),
            P("tvoc", "svoc", None, None, None),
            P("tvoc", "svoc", None, None),
            P("tvoc", "svoc"),
            P("dp", None),
            P(None, ("tvoc", "svoc")),
        ),
        out_specs=(P("dp"), P("dp", ("tvoc", "svoc")), P("dp", ("tvoc", "svoc"))),
        check_vma=False,
    )
```

profile of v0, /device:TPU:0, one launch (start us, length us, event | category | flops | bytes accessed | tf_op | source)
XLA Modules:
  0.0 32.7 jit_solution(5182986100618763320)
XLA Ops:
  1.3 30.2 %shard_map.85 = (f32[1,128]{1,0:T(1,128)S(1)}, bf16[1536,512]{1,0:T(8,128)(2,1)S(1)}, f32[192,128]{1,0:T(8,128)S(1)}) custom-call(s32[1,1,2,24]{3,2,1,0:T(2,128)} %bitcast.3, s32[1,1]{1,0:T(1,128)S(6)} %copy.9.cnt_s, bf16[128,5120]{1,0:T(8,128)(2,1)} %teacher_hbm.1, bf16[1,1,24,128,128]{4,3,2,1,0:T(8,128)(2,1)} %values_hbm.1, bf16[128,3072]{1,0:T(8,128)(2,1)} %hidden_hbm.1, ...), custom_call_target="tpu_custom_call" | custom-call | tf_op jit(solution)/shard_map/pallas_call | solution.py:386
  31.5 1.2 %shard_map.86 = (f32[1,128]{1,0:T(1,128)}, bf16[1536,512]{1,0:T(8,128)(2,1)}, f32[192,128]{1,0:T(8,128)}) custom-call(f32[1,128]{1,0:T(1,128)S(1)} %get-tuple-element.9.div, bf16[1536,512]{1,0:T(8,128)(2,1)S(1)} %get-tuple-element.10.gw, f32[192,128]{1,0:T(8,128)S(1)} %get-tuple-element.11.gh), custom_call_target="tpu_custom_call" | custom-call | tf_op jit(solution)/shard_map/pallas_call | solution.py:427
where the time goes:
time: 32.9 us; the launch traced here: 32.7 us
  Pallas kernels  31.4 us (95%)
  between operations  1.29 us (4%)
    pallas_call x1, Pallas kernels, local(): pl.pallas_call(functools.partial(kernel, n_t, n_s, blk), out_shape=(jax.S...  30.2 us
    pallas_call x1, Pallas kernels, local(): pl.pallas_call(flush, out_shape=tuple((jax.ShapeDtypeStruct(x.shape, x.dt...  1.19 us

commit v1 on v0

v1 whole, which is shorter than its diff:
```python
import functools

import jax
import jax.numpy as jnp
from jax import lax
from jax.experimental import pallas as pl
from jax.experimental.pallas import tpu as pltpu
from jax.sharding import PartitionSpec as P

loss_scale = 128.0
cap = 2
MESH = pl.DeviceIdType.MESH
f32, bf16 = jnp.float32, jnp.bfloat16


def split(n_t):
    n_lo = max(k for k in range(1, n_t + 1) if n_t % k == 0 and k * k <= n_t)
    return n_t // n_lo, n_lo


def kernel(
    n_t, n_s, blk,
    idx_hbm, cnt_hbm, teacher_hbm, values_hbm, hidden_hbm, weight_hbm,
    div_ref, gw_ref, gh_ref,
    idx_s, cnt_s, teacher, values, hidden, weight, peer_hidden, hid_t, mapped, targets, tags,
    packed, landed, mass, logits, shifted, stats, stats2, grads, grad_t, gh_t,
    own0, own1, hold0, hold1, out_a0, out_a1, rel0, rel1, out_b0, out_b1, fin0, fin1, out_z, in_z,
    load_sem, weight_sem, pair_sem, pk_send, pk_recv, st_send, st_recv, rs_send, rel_sem, fin_sem, z_recv,
):
    d, i, j = lax.axis_index("dp"), lax.axis_index("tvoc"), lax.axis_index("svoc")
    n_d = 2
    n = n_t * n_s
    n_hi, n_lo = split(n_t)
    me = i * n_s + j
    other = n_d - 1 - d
    tokens, width = hidden.shape
    shard = weight.shape[1]
    per_owner = shard // blk
    half = width // n_d
    rows = width // n
    slots = values.shape[0]

    barrier = pltpu.get_barrier_semaphore()

    def greet(q, carry):
        r = lax.rem(me + q, n)
        pl.semaphore_signal(
            barrier, inc=1, device_id={"tvoc": r // n_s, "svoc": lax.rem(r, n_s)}, device_id_type=MESH)
        return carry

    loads = [
        pltpu.make_async_copy(src, dst, load_sem.at[k])
        for k, (src, dst) in enumerate((
            (idx_hbm, idx_s), (cnt_hbm, cnt_s), (values_hbm.at[0, 0], values), (hidden_hbm, hidden)))
    ]
    parts = weight_sem.shape[0]
    depth = width // parts
    weight_loads = [
        pltpu.make_async_copy(
            weight_hbm.at[pl.ds(k * depth, depth)], weight.at[pl.ds(k * depth, depth)], weight_sem.at[k])
        for k in range(parts)
    ]
    blocks = teacher.shape[0]

    def block_start(b, carry):
        pltpu.make_async_copy(
            teacher_hbm.at[:, pl.ds(pl.multiple_of(b * blk, blk), blk)], teacher.at[b], load_sem.at[4]).start()
        return carry

    loads[0].start()
    loads[1].start()
    lax.fori_loop(1, n, greet, 0)
    pl.semaphore_signal(barrier, inc=1, device_id={"dp": other}, device_id_type=MESH)
    loads[2].start()
    lax.fori_loop(0, blocks, block_start, 0)
    loads[3].start()
    for copy in weight_loads:
        copy.start()
    loads[0].wait()
    loads[1].wait()
    lanes = targets.shape[1]
    lane = lax.broadcasted_iota(jnp.int32, (slots, lanes), 1)
    slot = lax.broadcasted_iota(jnp.int32, (slots, lanes), 0)
    column = jnp.zeros((slots, lanes), jnp.int32)
    for s in range(slots):
        column = jnp.where(slot == s, idx_s[0, 0, 1, s], column)
    hot = (column == lane) & (slot < cnt_s[0, 0])
    present = jnp.max(jnp.where(hot, 1.0, 0.0), axis=0, keepdims=True)
    r_iota = lax.broadcasted_iota(jnp.int32, (lanes, lanes), 0).astype(f32)
    c_iota = lax.broadcasted_iota(jnp.int32, (lanes, lanes), 1).astype(f32)
    r_own = jnp.floor((r_iota + 0.5) / per_owner)
    c_own = jnp.floor((c_iota + 0.5) / per_owner)
    below = jnp.where((r_own == c_own) & (r_iota < c_iota), 1.0, 0.0)
    rank = jnp.dot(jnp.broadcast_to(present, (8, lanes)), below, preferred_element_type=f32)[0:1]
    place = cap * c_own[0:1] + rank
    goal = jnp.sum(jnp.where(hot, place + 1.0, 0.0), axis=1, keepdims=True) - 1.0
    targets[...] = jnp.broadcast_to(goal, (slots, lanes))
    n_tags = n_t * cap
    t_iota = lax.broadcasted_iota(jnp.int32, (n_tags, lanes), 0).astype(f32)
    within = c_iota[0:1] - per_owner * c_own[0:1]
    tag = jnp.sum(jnp.where((present > 0.0) & (place == t_iota), within + 1.0, 0.0), axis=1, keepdims=True) - 1.0
    tag_row = lax.broadcasted_iota(jnp.int32, (n_tags, tokens), 0)
    tag_lane = lax.broadcasted_iota(jnp.int32, (n_tags, tokens), 1)
    tags[...] = jnp.sum(jnp.where(tag_row == tag_lane, jnp.broadcast_to(tag, (n_tags, tokens)), 0.0), axis=0, keepdims=True)
    loads[2].wait()
    pltpu.make_async_copy(teacher, teacher, load_sem.at[4]).wait()
    for s in range(slots):
        mapped[s] = jnp.dot(teacher[idx_s[0, 0, 0, s]], values[s], preferred_element_type=f32)
    def pack(o, weighed):
        for k in range(cap):
            t = (o * cap + k).astype(f32)
            acc = jnp.zeros((tokens, blk), f32)
            for s in range(slots):
                acc = acc + jnp.where(targets[s:s + 1, 0:blk] == t, mapped[s], 0.0)
            rounded = acc.astype(bf16)
            packed[o, :, k * blk:(k + 1) * blk] = rounded
            weighed = weighed + rounded.astype(f32)
        return weighed

    weighed = lax.fori_loop(0, n_t, pack, jnp.zeros((tokens, blk), f32))
    mass_part = jnp.sum(weighed, axis=1, keepdims=True)
    loads[3].wait()
    for k in range(parts):
        weight_loads[k].wait()
        part = jnp.dot(
            hidden[:, k * depth:(k + 1) * depth], weight[k * depth:(k + 1) * depth, :], preferred_element_type=f32)
        logits[...] = part if k == 0 else logits[...] + part
    lg = logits[...]
    top = jnp.max(lg, axis=1, keepdims=True)
    e = jnp.exp(lg - top)
    e_sum = jnp.sum(e, axis=1, keepdims=True)
    shifted[...] = e

    spot = lax.broadcasted_iota(jnp.int32, (tokens, 128), 1)

    def as_rows(columns, height):
        wide = jnp.zeros((tokens, 128), f32)
        for k, part in enumerate(columns):
            wide = jnp.where(spot == k, part, wide)
        return wide.T[0:height]

    stats[me, 0:3] = as_rows((top, e_sum, mass_part), 3)
    stats[me, 3:4] = tags[...]
    pl.semaphore_wait(barrier, n)
    def to_all(ref, send, recv_near, recv_far):
        def start(ii, jj, recv):
            pltpu.make_async_remote_copy(
                src_ref=ref.at[me], dst_ref=ref.at[me], send_sem=send, recv_sem=recv,
                device_id={"tvoc": ii, "svoc": jj}, device_id_type=MESH).start()

        def far(p, carry):
            jj = lax.rem(j + p, n_s)

            def inner(q, c):
                start(lax.rem(i + q, n_t), jj, recv_far)
                return c

            return lax.fori_loop(0, n_t, inner, carry)

        def near(q, carry):
            start(lax.rem(i + q, n_t), j, recv_near)
            return carry

        lax.fori_loop(1, n_s, far, 0)
        lax.fori_loop(1, n_t, near, 0)

    to_all(stats, st_send.at[0], st_recv.at[0], st_recv.at[1])

    def packed_copy(o, src):
        return pltpu.make_async_remote_copy(
            src_ref=packed.at[o], dst_ref=landed.at[src],
            send_sem=pk_send, recv_sem=pk_recv.at[src],
            device_id={"tvoc": o}, device_id_type=MESH)

    def pack_send(q, carry):
        packed_copy(lax.rem(i + q, n_t), i).start()
        return carry

    lax.fori_loop(1, n_t, pack_send, 0)

    def hidden_copy():
        start = pl.multiple_of(other * half, blk)
        return pltpu.make_async_remote_copy(
            src_ref=hidden.at[:, pl.ds(start, half)], dst_ref=peer_hidden,
            send_sem=pair_sem.at[0], recv_sem=pair_sem.at[1],
            device_id={"dp": other}, device_id_type=MESH)

    hidden_copy().start()
    own_at = d * half

    def turn_own(k, carry):
        at = pl.multiple_of(k * blk, blk)
        tile = hidden[:, pl.ds(pl.multiple_of(own_at + at, blk), blk)].astype(f32)
        hid_t[pl.ds(at, blk), 0:tokens] = tile.T.astype(bf16)
        return carry

    lax.fori_loop(0, half // blk, turn_own, 0)
    hidden_copy().wait_recv()

    def turn_peer(k, carry):
        at = pl.multiple_of(k * blk, blk)
        hid_t[pl.ds(at, blk), tokens:2 * tokens] = peer_hidden[:, pl.ds(at, blk)].astype(f32).T.astype(bf16)
        return carry

    lax.fori_loop(0, half // blk, turn_peer, 0)
    def block_wait(ref, count, sem):
        pltpu.make_async_copy(ref.at[pl.ds(0, count)], ref.at[pl.ds(0, count)], sem).wait()

    block_wait(stats, n_t - 1, st_recv.at[0])
    def add_mass(ref, o, first):
        row = stats[o * n_s + j, 3:4]
        seat = lax.broadcasted_iota(jnp.int32, row.shape, 1)
        which = [
            jnp.sum(jnp.where(seat == i * cap + k, row, 0.0), axis=1, keepdims=True) for k in range(cap)
        ]
        for b in range(per_owner):
            acc = jnp.zeros((tokens, blk), f32) if first else mass[:, b * blk:(b + 1) * blk]
            for k in range(cap):
                part = ref[o, :, k * blk:(k + 1) * blk].astype(f32)
                acc = acc + jnp.where(which[k] == float(b), part, 0.0)
            mass[:, b * blk:(b + 1) * blk] = acc

    add_mass(packed, i, True)

    def take_mass(q, carry):
        o = lax.rem(i + q, n_t)
        packed_copy(o, o).wait_recv()
        add_mass(landed, o, False)
        return carry

    lax.fori_loop(1, n_t, take_mass, 0)
    block_wait(stats, n - n_t, st_recv.at[1])
    st = stats[...]
    largest = jnp.max(st, axis=0)[0:1]
    scale = jnp.exp(st[:, 0:1, :] - largest[None])
    line = lax.broadcasted_iota(jnp.int32, st.shape, 1)
    sums = jnp.sum(jnp.where(line == 1, st * scale, st), axis=0)
    total, mass_sum = sums[1:2], sums[2:3]
    rows8 = lax.broadcasted_iota(jnp.int32, (128, tokens), 0)
    back = jnp.where(rows8 == 0, largest, jnp.where(rows8 == 1, loss_scale / total, loss_scale / mass_sum)).T
    factor = jnp.exp(top - back[:, 0:1]) * back[:, 1:2]
    g = shifted[...] * factor - mass[...] * back[:, 2:3]
    grads[0:tokens, :] = g.astype(bf16)
    lg_copy = pltpu.make_async_remote_copy(
        src_ref=grads.at[pl.ds(0, tokens)], dst_ref=grads.at[pl.ds(tokens, tokens)],
        send_sem=pair_sem.at[2], recv_sem=pair_sem.at[3],
        device_id={"dp": other}, device_id_type=MESH)
    lg_copy.start()
    grad_t[...] = g.T.astype(bf16)
    direct = rows % 16 == 0
    if not direct:
        tile = 2 * blk

        def gh_step(k, carry):
            at = pl.multiple_of(k * tile, tile)
            gh_t[pl.ds(at, tile), :] = jnp.dot(weight[pl.ds(at, tile), :], grad_t[...], preferred_element_type=f32)
            return carry

        lax.fori_loop(0, width // tile, gh_step, 0)

    def chunk(ii, jj):
        start = (ii * n_s + jj) * rows
        if not direct:
            return gh_t[pl.ds(pl.multiple_of(start, 8), rows), :]
        return jnp.dot(weight[pl.ds(pl.multiple_of(start, 16), rows), :], grad_t[...], preferred_element_type=f32)

    hi, lo = i // n_lo, lax.rem(i, n_lo)
    sizes = ((n_lo, n_hi), (n_hi, n_lo))
    cut = own0.shape[1]
    own, hold = (own0, own1), (hold0, hold1)
    out_a, rel = (out_a0, out_a1), (rel0, rel1)
    out_b, fin = (out_b0, out_b1), (fin0, fin1)

    def at_lo(q):
        return hi * n_lo + lax.rem(lo + q, n_lo)

    def at_hi(r):
        return lax.rem(hi + r, n_hi) * n_lo + lo

    def first(h, q):
        return at_lo(q) if h == 0 else at_hi(q)

    def second(h, r):
        return at_hi(r) if h == 0 else at_lo(r)

    def order(p):
        if p == n_s - 1:
            return j
        above = n_s - 1 - j
        low = jnp.where(p < above, n_s - 1 - p, p - above)
        high = jnp.where(p < j, p, n_s - 1 - (p - j))
        return jnp.where(2 * j < n_s, low, high)

    def relay_in(h, p, q, r):
        return pltpu.make_async_remote_copy(
            src_ref=out_a[h].at[p, q - 1, r], dst_ref=rel[h].at[p, q - 1, r - 1],
            send_sem=rs_send.at[h], recv_sem=rel_sem.at[h, p],
            device_id={"tvoc": first(h, q)}, device_id_type=MESH)

    def keep_in(h, p, q):
        return pltpu.make_async_remote_copy(
            src_ref=out_a[h].at[p, q - 1, 0], dst_ref=fin[h].at[p, q - 1],
            send_sem=rs_send.at[h], recv_sem=fin_sem.at[h, p],
            device_id={"tvoc": first(h, q)}, device_id_type=MESH)

    def relay_out(h, p, r):
        return pltpu.make_async_remote_copy(
            src_ref=out_b[h].at[p, r - 1], dst_ref=fin[h].at[p, sizes[h][0] - 2 + r],
            send_sem=rs_send.at[2 + h], recv_sem=fin_sem.at[h, p],
            device_id={"tvoc": second(h, r)}, device_id_type=MESH)

    def whole_wait(ref, sem):
        pltpu.make_async_copy(ref, ref, sem).wait()

    def dots(p):
        jj = order(p)
        for q in reversed(range(n_lo)):
            for r in reversed(range(n_hi)):
                ii = lax.rem(hi + r, n_hi) * n_lo + lax.rem(lo + q, n_lo)
                both = chunk(ii, jj)
                for h, (a, b) in enumerate(((q, r), (r, q))):
                    value = both[0:cut] if h == 0 else both[cut:]
                    if a:
                        out_a[h][p, a - 1, b] = value.astype(bf16)
                        (relay_in(h, p, a, b) if b else keep_in(h, p, a)).start()
                    elif b:
                        hold[h][p, b - 1] = value
                    else:
                        own[h][p] = value

    def relay(p):
        for h in range(2):
            n_a, n_b = sizes[h]
            if n_a == 1 or n_b == 1:
                if n_b > 1:
                    for r in range(1, n_b):
                        out_b[h][p, r - 1] = hold[h][p, r - 1].astype(bf16)
                        relay_out(h, p, r).start()
                continue
            whole_wait(rel[h].at[p], rel_sem.at[h, p])
            for r in range(1, n_b):
                acc = hold[h][p, r - 1]
                for q in range(1, n_a):
                    acc = acc + rel[h][p, q - 1, r - 1].astype(f32)
                out_b[h][p, r - 1] = acc.astype(bf16)
                relay_out(h, p, r).start()

    def gather(p, h):
        whole_wait(fin[h].at[p], fin_sem.at[h, p])
        acc = own[h][p]
        for k in range(fin[h].shape[1]):
            acc = acc + fin[h][p, k].astype(f32)
        return acc

    def finish(p):
        jj = order(p)
        out_z[p, 0:cut] = gather(p, 0).astype(bf16)
        out_z[p, cut:] = gather(p, 1).astype(bf16)
        pltpu.make_async_remote_copy(
            src_ref=out_z.at[p], dst_ref=in_z.at[lax.rem(j - jj + n_s, n_s) - 1],
            send_sem=rs_send.at[4], recv_sem=z_recv,
            device_id={"svoc": jj}, device_id_type=MESH).start()

    tall = 2 * blk
    tiles = half // tall
    done = [0]

    def gw_step(k, carry):
        at = pl.multiple_of(k * tall, tall)
        gw_ref[pl.ds(at, tall), :] = jnp.dot(
            hid_t[pl.ds(at, tall), :], grads[...], preferred_element_type=f32).astype(bf16)
        return carry

    def fill(count):
        until = min(tiles, done[0] + count)
        lax.fori_loop(done[0], until, gw_step, 0)
        done[0] = until

    for p in range(n_s):
        dots(p)
        if p >= 1 and p < n_s - 1:
            relay(p - 1)
    tm = mass[...]
    positive = tm > 0
    stats2[me] = as_rows((
        jnp.sum(jnp.where(positive, tm * jnp.log(jnp.where(positive, tm, 1.0)), 0.0), axis=1, keepdims=True),
        jnp.sum(tm * logits[...], axis=1, keepdims=True)), 2)
    to_all(stats2, st_send.at[1], st_recv.at[2], st_recv.at[2])
    for p in range(n_s - 3):
        finish(p)
    if n_s >= 2:
        relay(n_s - 2)
    lg_copy.wait_recv()
    fill(2)
    if n_s >= 3:
        finish(n_s - 3)
    relay(n_s - 1)
    fill(2)
    if n_s >= 2:
        finish(n_s - 2)
    fill(tiles)
    block_wait(stats2, n - 1, st_recv.at[2])
    late = jnp.sum(stats2[...], axis=0)
    entropy, cross = late[0:1], late[1:2]
    div_ref[...] = entropy / mass_sum - jnp.log(mass_sum) - cross / mass_sum + largest + jnp.log(total)
    mine = [gather(n_s - 1, h) for h in range(2)]
    whole_wait(in_z, z_recv)
    for h, (start, stop) in enumerate(((0, cut), (cut, rows))):
        acc = mine[h]
        for k in range(n_s - 1):
            acc = acc + in_z[k, start:stop].astype(f32)
        gh_ref[start:stop] = acc
    hidden_copy().wait_send()
    lg_copy.wait_send()
    block_wait(packed, n_t - 1, pk_send)
    block_wait(stats, n - 1, st_send.at[0])
    block_wait(stats2, n - 1, st_send.at[1])
    for h in range(2):
        whole_wait(out_a[h], rs_send.at[h])
        whole_wait(out_b[h], rs_send.at[2 + h])
    whole_wait(out_z, rs_send.at[4])


def flush(div, gw, gh, div_out, gw_out, gh_out, sem):
    copies = [
        pltpu.make_async_copy(src, dst, sem.at[k])
        for k, (src, dst) in enumerate(((gw, gw_out), (gh, gh_out), (div, div_out)))
    ]
    for copy in copies:
        copy.start()
    for copy in copies:
        copy.wait()


def local(n_t, n_s, teacher_probs, block_values, block_index, block_count, hidden, student_weight):
    tokens, width = hidden.shape
    slots, blk = block_values.shape[2], block_values.shape[3]
    shard = student_weight.shape[1]
    half, rows, n = width // 2, width // (n_t * n_s), n_t * n_s
    n_hi, n_lo = split(n_t)
    direct = rows % 16 == 0
    cut = -(-(rows // 2) // 16) * 16
    cuts = (cut, rows - cut)
    sizes = ((n_lo, n_hi), (n_hi, n_lo))
    lanes = -(-(n_t * (shard // blk)) // 128) * 128
    vmem = pl.BlockSpec(memory_space=pltpu.VMEM)
    hbm = pl.BlockSpec(memory_space=pltpu.HBM)
    DMA = pltpu.SemaphoreType.DMA
    parcel = (n_t, tokens, cap * blk)
    V = pltpu.VMEM
    relays = [
        *(V((n_s, c, tokens), f32) for c in cuts),
        *(V((n_s, b - 1, c, tokens), f32) for c, (a, b) in zip(cuts, sizes)),
        *(V((n_s, a - 1, b, c, tokens), bf16) for c, (a, b) in zip(cuts, sizes)),
        *(V((n_s, a - 1, b - 1, c, tokens), bf16) for c, (a, b) in zip(cuts, sizes)),
        *(V((n_s, b - 1, c, tokens), bf16) for c, (a, b) in zip(cuts, sizes)),
        *(V((n_s, a + b - 2, c, tokens), bf16) for c, (a, b) in zip(cuts, sizes)),
        V((n_s - 1, rows, tokens), bf16),
        V((n_s - 1, rows, tokens), bf16),
    ]
    parts = 3 if width % (3 * 128) == 0 else 1
    div, gw, gh = pl.pallas_call(
        functools.partial(kernel, n_t, n_s, blk),
        out_shape=(
            jax.ShapeDtypeStruct((1, tokens), f32),
            jax.ShapeDtypeStruct((half, shard), bf16),
            jax.ShapeDtypeStruct((rows, tokens), f32),
        ),
        in_specs=[hbm] * 6,
        out_specs=(vmem, vmem, vmem),
        scratch_shapes=[
            pltpu.SMEM((1, 1, 2, slots), jnp.int32),
            pltpu.SMEM((1, 1), jnp.int32),
            V((teacher_probs.shape[1] // blk, tokens, blk), bf16),
            V(block_values.shape[2:], bf16),
            V(hidden.shape, bf16),
            V(student_weight.shape, bf16),
            V((tokens, half), bf16),
            V((half, 2 * tokens), bf16),
            V((slots, tokens, blk), f32),
            V((slots, lanes), f32),
            V((1, tokens), f32),
            V(parcel, bf16),
            V(parcel, bf16),
            V((tokens, shard), f32),
            V((tokens, shard), f32),
            V((tokens, shard), f32),
            V((n, 4, tokens), f32),
            V((n, 2, tokens), f32),
            V((2 * tokens, shard), bf16),
            V((shard, tokens), bf16),
            V((8, 128) if direct else (width, tokens), f32),
            *relays,
            DMA((5,)), DMA((parts,)), DMA((4,)), DMA, DMA((n_t,)), DMA((2,)), DMA((3,)),
            DMA((5,)), DMA((2, n_s)), DMA((2, n_s)), DMA,
        ],
        compiler_params=pltpu.CompilerParams(
            collective_id=0, has_side_effects=True, vmem_limit_bytes=32 * 1024 * 1024),
    )(
        pltpu.with_memory_space_constraint(jnp.swapaxes(block_index, 2, 3), pltpu.HBM), block_count,
        *(pltpu.with_memory_space_constraint(x, pltpu.HBM) for x in (teacher_probs, block_values, hidden, student_weight)))
    div, gw, gh = pl.pallas_call(
        flush,
        out_shape=tuple(jax.ShapeDtypeStruct(x.shape, x.dtype) for x in (div, gw, gh)),
        in_specs=[vmem] * 3,
        out_specs=(hbm,) * 3,
        scratch_shapes=[DMA((3,))],
        compiler_params=pltpu.CompilerParams(vmem_limit_bytes=2**20),
    )(div, gw, gh)
    return div.reshape(tokens), gw, gh.T


def solution(mesh):
    return jax.shard_map(
        functools.partial(local, mesh.shape["tvoc"], mesh.shape["svoc"]),
        mesh=mesh,
        in_specs=(
            P("dp", "tvoc"),
            P("tvoc", "svoc", None, None, None),
            P("tvoc", "svoc", None, None),
            P("tvoc", "svoc"),
            P("dp", None),
            P(None, ("tvoc", "svoc")),
        ),
        out_specs=(P("dp"), P("dp", ("tvoc", "svoc")), P("dp", ("tvoc", "svoc"))),
        check_vma=False,
    )
```

time: 32.9 us -> 28.8 us (0.88)
  Pallas kernels: 31.4 us -> 27.3 us
    pallas_call x1, Pallas kernels: 30.2 us -> 26.2 us  [local(): pl.pallas_call(functools.partial(kernel, n_t, n_s, blk), out_shape=(jax.S...]
where the time goes in v1:
time: 28.8 us; the launch traced here: 28.6 us
  Pallas kernels  27.3 us (95%)
  between operations  1.29 us (4%)
    pallas_call x1, Pallas kernels, local(): pl.pallas_call(functools.partial(kernel, n_t, n_s, blk), out_shape=(jax.S...  26.2 us
    pallas_call x1, Pallas kernels, local(): pl.pallas_call(flush, out_shape=tuple((jax.ShapeDtypeStruct(x.shape, x.dt...  1.19 us

profile of v1, /device:TPU:0, one launch (start us, length us, event | category | flops | bytes accessed | tf_op | source)
XLA Modules:
  0.0 28.6 jit_solution(13467589432236359632)
XLA Ops:
  1.3 26.2 %shard_map.85 = (f32[1,128]{1,0:T(1,128)S(1)}, bf16[1536,512]{1,0:T(8,128)(2,1)S(1)}, f32[192,128]{1,0:T(8,128)S(1)}) custom-call(s32[1,1,2,24]{3,2,1,0:T(2,128)} %bitcast.3, s32[1,1]{1,0:T(1,128)S(6)} %copy.9.cnt_hbm, bf16[128,5120]{1,0:T(8,128)(2,1)} %teacher_hbm.1, bf16[1,1,24,128,128]{4,3,2,1,0:T(8,128)(2,1)} %values_hbm.1, ...), custom_call_target="tpu_custom_call" | custom-call | tf_op jit(solution)/shard_map/pallas_call | solution.py:462
  27.4 1.2 %shard_map.86 = (f32[1,128]{1,0:T(1,128)}, bf16[1536,512]{1,0:T(8,128)(2,1)}, f32[192,128]{1,0:T(8,128)}) custom-call(f32[1,128]{1,0:T(1,128)S(1)} %get-tuple-element.9.div, bf16[1536,512]{1,0:T(8,128)(2,1)S(1)} %get-tuple-element.10.gw, f32[192,128]{1,0:T(8,128)S(1)} %get-tuple-element.11.gh), custom_call_target="tpu_custom_call" | custom-call | tf_op jit(solution)/shard_map/pallas_call | solution.py:502

commit v2 on v1

--- a/solution.py
+++ b/solution.py
@@ -22,10 +22,10 @@
     n_t, n_s, blk,
     idx_hbm, cnt_hbm, teacher_hbm, values_hbm, hidden_hbm, weight_hbm,
     div_ref, gw_ref, gh_ref,
-    idx_s, cnt_s, teacher, values, hidden, weight, peer_hidden, hid_t, mapped, targets, tags,
+    idx_s, cnt_s, teacher, values, hidden, weight, peer_hidden, hid_t, mapped, keeps, tags, plan, plan_s,
     packed, landed, mass, logits, shifted, stats, stats2, grads, grad_t, gh_t,
-    own0, own1, hold0, hold1, out_a0, out_a1, rel0, rel1, out_b0, out_b1, fin0, fin1, out_z, in_z,
-    load_sem, weight_sem, pair_sem, pk_send, pk_recv, st_send, st_recv, rs_send, rel_sem, fin_sem, z_recv,
+    own, own_mate, hold, out, out_pair, out_mate, fin, fin_mate, in_z, in_pair, in_mate,
+    load_sem, weight_sem, pair_sem, pk_send, pk_recv, st_send, st_recv, rs_send, fin_sem, z_recv, pair_recv, mate_recv,
 ):
     d, i, j = lax.axis_index("dp"), lax.axis_index("tvoc"), lax.axis_index("svoc")
     n_d = 2
@@ -67,24 +67,25 @@
             teacher_hbm.at[:, pl.ds(pl.multiple_of(b * blk, blk), blk)], teacher.at[b], load_sem.at[4]).start()
         return carry
 
+    loads[2].start()
     loads[0].start()
     loads[1].start()
+    loads[3].start()
     lax.fori_loop(1, n, greet, 0)
     pl.semaphore_signal(barrier, inc=1, device_id={"dp": other}, device_id_type=MESH)
-    loads[2].start()
     lax.fori_loop(0, blocks, block_start, 0)
-    loads[3].start()
     for copy in weight_loads:
         copy.start()
     loads[0].wait()
     loads[1].wait()
-    lanes = targets.shape[1]
+    lanes = keeps.shape[1]
     lane = lax.broadcasted_iota(jnp.int32, (slots, lanes), 1)
     slot = lax.broadcasted_iota(jnp.int32, (slots, lanes), 0)
     column = jnp.zeros((slots, lanes), jnp.int32)
     for s in range(slots):
         column = jnp.where(slot == s, idx_s[0, 0, 1, s], column)
-    hot = (column == lane) & (slot < cnt_s[0, 0])
+    live = slot < cnt_s[0, 0]
+    hot = (column == lane) & live
     present = jnp.max(jnp.where(hot, 1.0, 0.0), axis=0, keepdims=True)
     r_iota = lax.broadcasted_iota(jnp.int32, (lanes, lanes), 0).astype(f32)
     c_iota = lax.broadcasted_iota(jnp.int32, (lanes, lanes), 1).astype(f32)
@@ -93,26 +94,46 @@
     below = jnp.where((r_own == c_own) & (r_iota < c_iota), 1.0, 0.0)
     rank = jnp.dot(jnp.broadcast_to(present, (8, lanes)), below, preferred_element_type=f32)[0:1]
     place = cap * c_own[0:1] + rank
-    goal = jnp.sum(jnp.where(hot, place + 1.0, 0.0), axis=1, keepdims=True) - 1.0
-    targets[...] = jnp.broadcast_to(goal, (slots, lanes))
     n_tags = n_t * cap
     t_iota = lax.broadcasted_iota(jnp.int32, (n_tags, lanes), 0).astype(f32)
     within = c_iota[0:1] - per_owner * c_own[0:1]
-    tag = jnp.sum(jnp.where((present > 0.0) & (place == t_iota), within + 1.0, 0.0), axis=1, keepdims=True) - 1.0
-    tag_row = lax.broadcasted_iota(jnp.int32, (n_tags, tokens), 0)
-    tag_lane = lax.broadcasted_iota(jnp.int32, (n_tags, tokens), 1)
-    tags[...] = jnp.sum(jnp.where(tag_row == tag_lane, jnp.broadcast_to(tag, (n_tags, tokens)), 0.0), axis=0, keepdims=True)
+    named = (present > 0.0) & (place == t_iota)
+    tag_diag = lax.broadcasted_iota(jnp.int32, (n_tags, lanes), 0) == lax.broadcasted_iota(jnp.int32, (n_tags, lanes), 1)
+
+    def along(col):
+        return jnp.sum(jnp.where(tag_diag, jnp.broadcast_to(col, (n_tags, lanes)), 0.0), axis=0, keepdims=True)
+
+    tags[...] = along(jnp.sum(jnp.where(named, within + 1.0, 0.0), axis=1, keepdims=True) - 1.0)[:, 0:tokens]
+    upto = jnp.sum(jnp.where(live & (column <= lane), 1.0, 0.0), axis=0, keepdims=True)
+    last = jnp.sum(jnp.where(named, upto, 0.0), axis=1, keepdims=True)
+    last = jnp.where(last > 0.0, last - 1.0, float(slots))
+    slot_f, lane_f = slot.astype(f32), lane.astype(f32)
+    diag = slot == lane
+    key = jnp.where(live, column * slots, lanes * slots).astype(f32) + slot_f
+    key_row = jnp.sum(jnp.where(diag, key, 0.0), axis=0, keepdims=True)
+    key_row = jnp.where(lane_f[0:1] < slots, key_row, 2.0 * lanes * slots)
+    spot_of = jnp.sum(jnp.where(key_row < key, 1.0, 0.0), axis=1, keepdims=True)
+    here = spot_of == lane_f
+    plan[0:1] = jnp.sum(jnp.where(here, slot_f, 0.0), axis=0, keepdims=True).astype(jnp.int32)
+    plan[1:2] = along(last).astype(jnp.int32)
+    plan_copy = pltpu.make_async_copy(plan, plan_s, load_sem.at[5])
+    plan_copy.start()
+    sorted_row = jnp.sum(jnp.where(here, column.astype(f32), 0.0), axis=0, keepdims=True)
+    same = jnp.where(sorted_row == pltpu.roll(sorted_row, 1, 1), 1.0, 0.0)
+    keeps[...] = jnp.broadcast_to(jnp.sum(jnp.where(diag, same, 0.0), axis=1, keepdims=True), (slots, lanes))
+    mapped[slots] = jnp.zeros((tokens, blk), f32)
+    plan_copy.wait()
     loads[2].wait()
     pltpu.make_async_copy(teacher, teacher, load_sem.at[4]).wait()
-    for s in range(slots):
-        mapped[s] = jnp.dot(teacher[idx_s[0, 0, 0, s]], values[s], preferred_element_type=f32)
+    run = None
+    for k in range(slots):
+        s = jnp.clip(plan_s[0, k], 0, slots - 1)
+        term = jnp.dot(teacher[idx_s[0, 0, 0, s]], values[s], preferred_element_type=f32)
+        run = term if k == 0 else term + keeps[k:k + 1, 0:blk] * run
+        mapped[k] = run
     def pack(o, weighed):
         for k in range(cap):
-            t = (o * cap + k).astype(f32)
-            acc = jnp.zeros((tokens, blk), f32)
-            for s in range(slots):
-                acc = acc + jnp.where(targets[s:s + 1, 0:blk] == t, mapped[s], 0.0)
-            rounded = acc.astype(bf16)
+            rounded = mapped[jnp.clip(plan_s[1, o * cap + k], 0, slots)].astype(bf16)
             packed[o, :, k * blk:(k + 1) * blk] = rounded
             weighed = weighed + rounded.astype(f32)
         return weighed
@@ -166,6 +187,9 @@
 
     to_all(stats, st_send.at[0], st_recv.at[0], st_recv.at[1])
 
+    def spread(k):
+        return lax.rem(i // n_lo + lax.rem(k, n_hi), n_hi) * n_lo + lax.rem(i + k // n_hi, n_lo)
+
     def packed_copy(o, src):
         return pltpu.make_async_remote_copy(
             src_ref=packed.at[o], dst_ref=landed.at[src],
@@ -173,7 +197,7 @@
             device_id={"tvoc": o}, device_id_type=MESH)
 
     def pack_send(q, carry):
-        packed_copy(lax.rem(i + q, n_t), i).start()
+        packed_copy(spread(n_t - q), i).start()
         return carry
 
     lax.fori_loop(1, n_t, pack_send, 0)
@@ -223,7 +247,7 @@
     add_mass(packed, i, True)
 
     def take_mass(q, carry):
-        o = lax.rem(i + q, n_t)
+        o = spread(q)
         packed_copy(o, o).wait_recv()
         add_mass(landed, o, False)
         return carry
@@ -258,108 +282,90 @@
 
         lax.fori_loop(0, width // tile, gh_step, 0)
 
-    def chunk(ii, jj):
-        start = (ii * n_s + jj) * rows
+    def chunk(ii, jj, begin=0, end=rows):
+        start = (ii * n_s + jj) * rows + begin
         if not direct:
-            return gh_t[pl.ds(pl.multiple_of(start, 8), rows), :]
-        return jnp.dot(weight[pl.ds(pl.multiple_of(start, 16), rows), :], grad_t[...], preferred_element_type=f32)
+            return gh_t[pl.ds(pl.multiple_of(start, 8), end - begin), :]
+        return jnp.dot(
+            weight[pl.ds(pl.multiple_of(start, 16), end - begin), :], grad_t[...], preferred_element_type=f32)
 
     hi, lo = i // n_lo, lax.rem(i, n_lo)
-    sizes = ((n_lo, n_hi), (n_hi, n_lo))
-    cut = own0.shape[1]
-    own, hold = (own0, own1), (hold0, hold1)
-    out_a, rel = (out_a0, out_a1), (rel0, rel1)
-    out_b, fin = (out_b0, out_b1), (fin0, fin1)
-
-    def at_lo(q):
-        return hi * n_lo + lax.rem(lo + q, n_lo)
-
-    def at_hi(r):
-        return lax.rem(hi + r, n_hi) * n_lo + lo
-
-    def first(h, q):
-        return at_lo(q) if h == 0 else at_hi(q)
-
-    def second(h, r):
-        return at_hi(r) if h == 0 else at_lo(r)
+    early = in_pair.shape[1]
+    rest = rows - early
+
+    def place_of(k):
+        q, r = k // n_hi, k % n_hi
+        return lax.rem(hi + r, n_hi) * n_lo + lax.rem(lo + q, n_lo)
 
     def order(p):
         if p == n_s - 1:
             return j
-        above = n_s - 1 - j
-        low = jnp.where(p < above, n_s - 1 - p, p - above)
-        high = jnp.where(p < j, p, n_s - 1 - (p - j))
-        return jnp.where(2 * j < n_s, low, high)
-
-    def relay_in(h, p, q, r):
-        return pltpu.make_async_remote_copy(
-            src_ref=out_a[h].at[p, q - 1, r], dst_ref=rel[h].at[p, q - 1, r - 1],
-            send_sem=rs_send.at[h], recv_sem=rel_sem.at[h, p],
-            device_id={"tvoc": first(h, q)}, device_id_type=MESH)
-
-    def keep_in(h, p, q):
-        return pltpu.make_async_remote_copy(
-            src_ref=out_a[h].at[p, q - 1, 0], dst_ref=fin[h].at[p, q - 1],
-            send_sem=rs_send.at[h], recv_sem=fin_sem.at[h, p],
-            device_id={"tvoc": first(h, q)}, device_id_type=MESH)
-
-    def relay_out(h, p, r):
-        return pltpu.make_async_remote_copy(
-            src_ref=out_b[h].at[p, r - 1], dst_ref=fin[h].at[p, sizes[h][0] - 2 + r],
-            send_sem=rs_send.at[2 + h], recv_sem=fin_sem.at[h, p],
-            device_id={"tvoc": second(h, r)}, device_id_type=MESH)
+        if p == n_s - 2:
+            return j + 1 - 2 * lax.rem(j, 2)
+        pairs, jp, pp, member = n_s // 2, j // 2, p // 2, p % 2
+        above = pairs - 1 - jp
+        low = 2 * jnp.where(pp < above, pairs - 1 - pp, pp - above) + 1 - member
+        high = 2 * jnp.where(pp < jp, pp, pairs - 1 - (pp - jp)) + member
+        return jnp.where(2 * jp < pairs, low, high)
+
+    mate = order(n_s - 2)
+
+    def slot_of(jj):
+        return lax.rem(j // 2 - jj // 2 + n_s // 2, n_s // 2) * 2 - 2 + lax.rem(j, 2)
 
     def whole_wait(ref, sem):
         pltpu.make_async_copy(ref, ref, sem).wait()
 
-    def dots(p):
-        jj = order(p)
-        for q in reversed(range(n_lo)):
-            for r in reversed(range(n_hi)):
-                ii = lax.rem(hi + r, n_hi) * n_lo + lax.rem(lo + q, n_lo)
-                both = chunk(ii, jj)
-                for h, (a, b) in enumerate(((q, r), (r, q))):
-                    value = both[0:cut] if h == 0 else both[cut:]
-                    if a:
-                        out_a[h][p, a - 1, b] = value.astype(bf16)
-                        (relay_in(h, p, a, b) if b else keep_in(h, p, a)).start()
-                    elif b:
-                        hold[h][p, b - 1] = value
-                    else:
-                        own[h][p] = value
-
-    def relay(p):
-        for h in range(2):
-            n_a, n_b = sizes[h]
-            if n_a == 1 or n_b == 1:
-                if n_b > 1:
-                    for r in range(1, n_b):
-                        out_b[h][p, r - 1] = hold[h][p, r - 1].astype(bf16)
-                        relay_out(h, p, r).start()
-                continue
-            whole_wait(rel[h].at[p], rel_sem.at[h, p])
-            for r in range(1, n_b):
-                acc = hold[h][p, r - 1]
-                for q in range(1, n_a):
-                    acc = acc + rel[h][p, q - 1, r - 1].astype(f32)
-                out_b[h][p, r - 1] = acc.astype(bf16)
-                relay_out(h, p, r).start()
-
-    def gather(p, h):
-        whole_wait(fin[h].at[p], fin_sem.at[h, p])
-        acc = own[h][p]
-        for k in range(fin[h].shape[1]):
-            acc = acc + fin[h][p, k].astype(f32)
+    counts = [0, 0, 0]
+
+    def ship(kind, value, dst, recv, where):
+        src = (out, out_pair, out_mate)[kind].at[counts[kind]]
+        counts[kind] += 1
+        src[...] = value.astype(bf16)
+        pltpu.make_async_remote_copy(
+            src_ref=src, dst_ref=dst, send_sem=rs_send.at[kind], recv_sem=recv,
+            device_id=where, device_id_type=MESH).start()
+
+    def send_dots(p):
+        for k in reversed(range(1, n_t)):
+            ii = place_of(k)
+            if p == n_s - 2:
+                ship(2, chunk(ii, mate, early), fin_mate.at[k - 1], fin_sem.at[p], {"tvoc": ii})
+            else:
+                ship(0, chunk(ii, order(p)), fin.at[p, k - 1], fin_sem.at[p], {"tvoc": ii})
+
+    def pair_dots():
+        for k in reversed(range(n_t)):
+            ship(1, chunk(place_of(k), mate, 0, early), in_pair.at[k], pair_recv, {"svoc": mate})
+
+    def own_dots():
+        for k in reversed(range(n_t)):
+            hold[k] = chunk(place_of(k), j)
+
+    def own_send():
+        whole_wait(in_pair, pair_recv)
+        for k in reversed(range(n_t)):
+            hold[k, 0:early] = hold[k, 0:early] + in_pair[k].astype(f32)
+            if k:
+                ship(0, hold[k], fin.at[n_s - 1, k - 1], fin_sem.at[n_s - 1], {"tvoc": place_of(k)})
+
+    def gather(p):
+        if p == n_s - 2:
+            acc, terms = own_mate[...], fin_mate
+        else:
+            acc, terms = own[p] if p < n_s - 1 else hold[0], fin.at[p]
+        if n_t > 1:
+            whole_wait(terms, fin_sem.at[p])
+        for k in range(n_t - 1):
+            acc = acc + terms[k].astype(f32)
         return acc
 
     def finish(p):
         jj = order(p)
-        out_z[p, 0:cut] = gather(p, 0).astype(bf16)
-        out_z[p, cut:] = gather(p, 1).astype(bf16)
-        pltpu.make_async_remote_copy(
-            src_ref=out_z.at[p], dst_ref=in_z.at[lax.rem(j - jj + n_s, n_s) - 1],
-            send_sem=rs_send.at[4], recv_sem=z_recv,
-            device_id={"svoc": jj}, device_id_type=MESH).start()
+        if p == n_s - 2:
+            ship(2, gather(p), in_mate, mate_recv, {"svoc": jj})
+        else:
+            ship(0, gather(p), in_z.at[slot_of(jj)], z_recv, {"svoc": jj})
 
     tall = 2 * blk
     tiles = half // tall
@@ -376,49 +382,50 @@
         lax.fori_loop(done[0], until, gw_step, 0)
         done[0] = until
 
-    for p in range(n_s):
-        dots(p)
-        if p >= 1 and p < n_s - 1:
-            relay(p - 1)
-    tm = mass[...]
-    positive = tm > 0
-    stats2[me] = as_rows((
-        jnp.sum(jnp.where(positive, tm * jnp.log(jnp.where(positive, tm, 1.0)), 0.0), axis=1, keepdims=True),
-        jnp.sum(tm * logits[...], axis=1, keepdims=True)), 2)
-    to_all(stats2, st_send.at[1], st_recv.at[2], st_recv.at[2])
-    for p in range(n_s - 3):
+    def spread_late():
+        tm = mass[...]
+        positive = tm > 0
+        stats2[me] = as_rows((
+            jnp.sum(jnp.where(positive, tm * jnp.log(jnp.where(positive, tm, 1.0)), 0.0), axis=1, keepdims=True),
+            jnp.sum(tm * logits[...], axis=1, keepdims=True)), 2)
+        to_all(stats2, st_send.at[1], st_recv.at[2], st_recv.at[2])
+
+    for p in range(n_s - 2):
+        send_dots(p)
+        if p == 0:
+            pair_dots()
+    if n_s == 2:
+        pair_dots()
+    send_dots(n_s - 2)
+    for p in range(n_s - 2):
+        own[p] = chunk(i, order(p))
+    own_mate[...] = chunk(i, mate, early)
+    own_dots()
+    spread_late()
+    lg_copy.wait_recv()
+    fill(tiles)
+    own_send()
+    for p in range(n_s - 1):
         finish(p)
-    if n_s >= 2:
-        relay(n_s - 2)
-    lg_copy.wait_recv()
-    fill(2)
-    if n_s >= 3:
-        finish(n_s - 3)
-    relay(n_s - 1)
-    fill(2)
-    if n_s >= 2:
-        finish(n_s - 2)
-    fill(tiles)
     block_wait(stats2, n - 1, st_recv.at[2])
     late = jnp.sum(stats2[...], axis=0)
     entropy, cross = late[0:1], late[1:2]
     div_ref[...] = entropy / mass_sum - jnp.log(mass_sum) - cross / mass_sum + largest + jnp.log(total)
-    mine = [gather(n_s - 1, h) for h in range(2)]
-    whole_wait(in_z, z_recv)
-    for h, (start, stop) in enumerate(((0, cut), (cut, rows))):
-        acc = mine[h]
-        for k in range(n_s - 1):
-            acc = acc + in_z[k, start:stop].astype(f32)
-        gh_ref[start:stop] = acc
+    acc = gather(n_s - 1)
+    if n_s > 2:
+        whole_wait(in_z, z_recv)
+    for k in range(n_s - 2):
+        acc = acc + in_z[k].astype(f32)
+    gh_ref[0:early] = acc[0:early]
+    whole_wait(in_mate, mate_recv)
+    gh_ref[early:] = acc[early:] + in_mate[...].astype(f32)
     hidden_copy().wait_send()
     lg_copy.wait_send()
     block_wait(packed, n_t - 1, pk_send)
     block_wait(stats, n - 1, st_send.at[0])
     block_wait(stats2, n - 1, st_send.at[1])
-    for h in range(2):
-        whole_wait(out_a[h], rs_send.at[h])
-        whole_wait(out_b[h], rs_send.at[2 + h])
-    whole_wait(out_z, rs_send.at[4])
+    for kind, ref in enumerate((out, out_pair, out_mate)):
+        block_wait(ref, counts[kind], rs_send.at[kind])
 
 
 def flush(div, gw, gh, div_out, gw_out, gh_out, sem):
@@ -439,24 +446,26 @@
     half, rows, n = width // 2, width // (n_t * n_s), n_t * n_s
     n_hi, n_lo = split(n_t)
     direct = rows % 16 == 0
-    cut = -(-(rows // 2) // 16) * 16
-    cuts = (cut, rows - cut)
-    sizes = ((n_lo, n_hi), (n_hi, n_lo))
     lanes = -(-(n_t * (shard // blk)) // 128) * 128
     vmem = pl.BlockSpec(memory_space=pltpu.VMEM)
     hbm = pl.BlockSpec(memory_space=pltpu.HBM)
     DMA = pltpu.SemaphoreType.DMA
     parcel = (n_t, tokens, cap * blk)
     V = pltpu.VMEM
-    relays = [
-        *(V((n_s, c, tokens), f32) for c in cuts),
-        *(V((n_s, b - 1, c, tokens), f32) for c, (a, b) in zip(cuts, sizes)),
-        *(V((n_s, a - 1, b, c, tokens), bf16) for c, (a, b) in zip(cuts, sizes)),
-        *(V((n_s, a - 1, b - 1, c, tokens), bf16) for c, (a, b) in zip(cuts, sizes)),
-        *(V((n_s, b - 1, c, tokens), bf16) for c, (a, b) in zip(cuts, sizes)),
-        *(V((n_s, a + b - 2, c, tokens), bf16) for c, (a, b) in zip(cuts, sizes)),
-        V((n_s - 1, rows, tokens), bf16),
-        V((n_s - 1, rows, tokens), bf16),
+    early = -(-(rows // 2) // 16) * 16
+    rest = rows - early
+    exchange = [
+        V((n_s - 1, rows, tokens), f32),
+        V((rest, tokens), f32),
+        V((n_t, rows, tokens), f32),
+        V((n_s * n_t, rows, tokens), bf16),
+        V((n_t, early, tokens), bf16),
+        V((n_t, rest, tokens), bf16),
+        V((n_s, n_t - 1, rows, tokens), bf16),
+        V((n_t - 1, rest, tokens), bf16),
+        V((max(n_s - 2, 1), rows, tokens), bf16),
+        V((n_t, early, tokens), bf16),
+        V((rest, tokens), bf16),
     ]
     parts = 3 if width % (3 * 128) == 0 else 1
     div, gw, gh = pl.pallas_call(
@@ -477,9 +486,11 @@
             V(student_weight.shape, bf16),
             V((tokens, half), bf16),
             V((half, 2 * tokens), bf16),
-            V((slots, tokens, blk), f32),
+            V((slots + 1, tokens, blk), f32),
             V((slots, lanes), f32),
             V((1, tokens), f32),
+            V((2, lanes), jnp.int32),
+            pltpu.SMEM((2, lanes), jnp.int32),
             V(parcel, bf16),
             V(parcel, bf16),
             V((tokens, shard), f32),
@@ -490,9 +501,9 @@
             V((2 * tokens, shard), bf16),
             V((shard, tokens), bf16),
             V((8, 128) if direct else (width, tokens), f32),
-            *relays,
-            DMA((5,)), DMA((parts,)), DMA((4,)), DMA, DMA((n_t,)), DMA((2,)), DMA((3,)),
-            DMA((5,)), DMA((2, n_s)), DMA((2, n_s)), DMA,
+            *exchange,
+            DMA((6,)), DMA((parts,)), DMA((4,)), DMA, DMA((n_t,)), DMA((2,)), DMA((3,)),
+            DMA((3,)), DMA((n_s,)), DMA, DMA, DMA,
         ],
         compiler_params=pltpu.CompilerParams(
             collective_id=0, has_side_effects=True, vmem_limit_bytes=32 * 1024 * 1024),

time: 28.8 us -> 26.2 us (0.910)
  Pallas kernels: 27.3 us -> 24.8 us
    pallas_call x1, Pallas kernels: 26.2 us -> 23.6 us  [local(): pl.pallas_call(functools.partial(kernel, n_t, n_s, blk), out_shape=(jax.S...]
where the time goes in v2:
time: 26.2 us; the launch traced here: 26.1 us
  Pallas kernels  24.8 us (95%)
  between operations  1.29 us (5%)
    pallas_call x1, Pallas kernels, local(): pl.pallas_call(functools.partial(kernel, n_t, n_s, blk), out_shape=(jax.S...  23.6 us
    pallas_call x1, Pallas kernels, local(): pl.pallas_call(flush, out_shape=tuple((jax.ShapeDtypeStruct(x.shape, x.dt...  1.19 us

profile of v2, /device:TPU:0, one launch (start us, length us, event | category | flops | bytes accessed | tf_op | source)
XLA Modules:
  0.0 26.1 jit_solution(3776955395668514572)
XLA Ops:
  1.3 23.6 %shard_map.85 = (f32[1,128]{1,0:T(1,128)S(1)}, bf16[1536,512]{1,0:T(8,128)(2,1)S(1)}, f32[192,128]{1,0:T(8,128)S(1)}) custom-call(s32[1,1,2,24]{3,2,1,0:T(2,128)} %bitcast.3, s32[1,1]{1,0:T(1,128)S(6)} %copy.9.cnt_hbm, bf16[128,5120]{1,0:T(8,128)(2,1)} %teacher_hbm.1, bf16[1,1,24,128,128]{4,3,2,1,0:T(8,128)(2,1)} %values_hbm.1, ...), custom_call_target="tpu_custom_call" | custom-call | tf_op jit(solution)/shard_map/pallas_call | solution.py:471
  24.9 1.2 %shard_map.86 = (f32[1,128]{1,0:T(1,128)}, bf16[1536,512]{1,0:T(8,128)(2,1)}, f32[192,128]{1,0:T(8,128)}) custom-call(f32[1,128]{1,0:T(1,128)S(1)} %get-tuple-element.9.div, bf16[1536,512]{1,0:T(8,128)(2,1)S(1)} %get-tuple-element.10.gw, f32[192,128]{1,0:T(8,128)S(1)} %get-tuple-element.11.gh), custom_call_target="tpu_custom_call" | custom-call | tf_op jit(solution)/shard_map/pallas_call | solution.py:513

commit v3 on v2

--- a/solution.py
+++ b/solution.py
@@ -23,7 +23,7 @@
     idx_hbm, cnt_hbm, teacher_hbm, values_hbm, hidden_hbm, weight_hbm,
     div_ref, gw_ref, gh_ref,
     idx_s, cnt_s, teacher, values, hidden, weight, peer_hidden, hid_t, mapped, keeps, tags, plan, plan_s,
-    packed, landed, mass, logits, shifted, stats, stats2, grads, grad_t, gh_t,
+    packed, landed, mass, logits, shifted, tops, stats, stats2, grads, grad_t, gh_t,
     own, own_mate, hold, out, out_pair, out_mate, fin, fin_mate, in_z, in_pair, in_mate,
     load_sem, weight_sem, pair_sem, pk_send, pk_recv, st_send, st_recv, rs_send, fin_sem, z_recv, pair_recv, mate_recv,
 ):
@@ -140,18 +140,6 @@
 
     weighed = lax.fori_loop(0, n_t, pack, jnp.zeros((tokens, blk), f32))
     mass_part = jnp.sum(weighed, axis=1, keepdims=True)
-    loads[3].wait()
-    for k in range(parts):
-        weight_loads[k].wait()
-        part = jnp.dot(
-            hidden[:, k * depth:(k + 1) * depth], weight[k * depth:(k + 1) * depth, :], preferred_element_type=f32)
-        logits[...] = part if k == 0 else logits[...] + part
-    lg = logits[...]
-    top = jnp.max(lg, axis=1, keepdims=True)
-    e = jnp.exp(lg - top)
-    e_sum = jnp.sum(e, axis=1, keepdims=True)
-    shifted[...] = e
-
     spot = lax.broadcasted_iota(jnp.int32, (tokens, 128), 1)
 
     def as_rows(columns, height):
@@ -160,9 +148,38 @@
             wide = jnp.where(spot == k, part, wide)
         return wide.T[0:height]
 
-    stats[me, 0:3] = as_rows((top, e_sum, mass_part), 3)
-    stats[me, 3:4] = tags[...]
+    def softmax():
+        loads[3].wait()
+        for k in range(parts):
+            weight_loads[k].wait()
+            part = jnp.dot(
+                hidden[:, k * depth:(k + 1) * depth], weight[k * depth:(k + 1) * depth, :], preferred_element_type=f32)
+            logits[...] = part if k == 0 else logits[...] + part
+        lg = logits[...]
+        top = jnp.max(lg, axis=1, keepdims=True)
+        e = jnp.exp(lg - top)
+        shifted[...] = e
+        tops[...] = jnp.broadcast_to(top, tops.shape)
+        stats[me, 0:3] = as_rows((top, jnp.sum(e, axis=1, keepdims=True), mass_part), 3)
+        stats[me, 3:4] = tags[...]
+
+    pl.when(j == 0)(softmax)
     pl.semaphore_wait(barrier, n)
+    def spread(k):
+        return lax.rem(i // n_lo + lax.rem(k, n_hi), n_hi) * n_lo + lax.rem(i + k // n_hi, n_lo)
+
+    def packed_copy(o, src):
+        return pltpu.make_async_remote_copy(
+            src_ref=packed.at[o], dst_ref=landed.at[src],
+            send_sem=pk_send, recv_sem=pk_recv.at[src],
+            device_id={"tvoc": o}, device_id_type=MESH)
+
+    near = [k for k in range(1, n_t) if k % n_hi == 0 or k < n_hi]
+    away = [k for k in range(1, n_t) if k not in near]
+    for k in near:
+        packed_copy(spread(k), i).start()
+
+    pl.when(j != 0)(softmax)
     def to_all(ref, send, recv_near, recv_far):
         def start(ii, jj, recv):
             pltpu.make_async_remote_copy(
@@ -186,21 +203,8 @@
         lax.fori_loop(1, n_t, near, 0)
 
     to_all(stats, st_send.at[0], st_recv.at[0], st_recv.at[1])
-
-    def spread(k):
-        return lax.rem(i // n_lo + lax.rem(k, n_hi), n_hi) * n_lo + lax.rem(i + k // n_hi, n_lo)
-
-    def packed_copy(o, src):
-        return pltpu.make_async_remote_copy(
-            src_ref=packed.at[o], dst_ref=landed.at[src],
-            send_sem=pk_send, recv_sem=pk_recv.at[src],
-            device_id={"tvoc": o}, device_id_type=MESH)
-
-    def pack_send(q, carry):
-        packed_copy(spread(n_t - q), i).start()
-        return carry
-
-    lax.fori_loop(1, n_t, pack_send, 0)
+    for k in away:
+        packed_copy(spread(k), i).start()
 
     def hidden_copy():
         start = pl.multiple_of(other * half, blk)
@@ -262,7 +266,7 @@
     total, mass_sum = sums[1:2], sums[2:3]
     rows8 = lax.broadcasted_iota(jnp.int32, (128, tokens), 0)
     back = jnp.where(rows8 == 0, largest, jnp.where(rows8 == 1, loss_scale / total, loss_scale / mass_sum)).T
-    factor = jnp.exp(top - back[:, 0:1]) * back[:, 1:2]
+    factor = jnp.exp(tops[:, 0:1] - back[:, 0:1]) * back[:, 1:2]
     g = shifted[...] * factor - mass[...] * back[:, 2:3]
     grads[0:tokens, :] = g.astype(bf16)
     lg_copy = pltpu.make_async_remote_copy(
@@ -390,13 +394,11 @@
             jnp.sum(tm * logits[...], axis=1, keepdims=True)), 2)
         to_all(stats2, st_send.at[1], st_recv.at[2], st_recv.at[2])
 
-    for p in range(n_s - 2):
+    turns = [*range(min(1, n_s - 2)), n_s - 2, *range(1, n_s - 2)]
+    for p in turns:
+        if p == n_s - 2:
+            pair_dots()
         send_dots(p)
-        if p == 0:
-            pair_dots()
-    if n_s == 2:
-        pair_dots()
-    send_dots(n_s - 2)
     for p in range(n_s - 2):
         own[p] = chunk(i, order(p))
     own_mate[...] = chunk(i, mate, early)
@@ -405,7 +407,7 @@
     lg_copy.wait_recv()
     fill(tiles)
     own_send()
-    for p in range(n_s - 1):
+    for p in turns:
         finish(p)
     block_wait(stats2, n - 1, st_recv.at[2])
     late = jnp.sum(stats2[...], axis=0)
@@ -496,6 +498,7 @@
             V((tokens, shard), f32),
             V((tokens, shard), f32),
             V((tokens, shard), f32),
+            V((tokens, 128), f32),
             V((n, 4, tokens), f32),
             V((n, 2, tokens), f32),
             V((2 * tokens, shard), bf16),

time: 26.2 us -> 25.2 us (0.962)
  Pallas kernels: 24.8 us -> 23.7 us
    pallas_call x1, Pallas kernels: 23.6 us -> 22.5 us  [local(): pl.pallas_call(functools.partial(kernel, n_t, n_s, blk), out_shape=(jax.S...]
where the time goes in v3:
time: 25.2 us; the launch traced here: 25 us
  Pallas kernels  23.7 us (94%)
  between operations  1.29 us (5%)
    pallas_call x1, Pallas kernels, local(): pl.pallas_call(functools.partial(kernel, n_t, n_s, blk), out_shape=(jax.S...  22.5 us
    pallas_call x1, Pallas kernels, local(): pl.pallas_call(flush, out_shape=tuple((jax.ShapeDtypeStruct(x.shape, x.dt...  1.19 us

profile of v3, /device:TPU:0, one launch (start us, length us, event | category | flops | bytes accessed | tf_op | source)
XLA Modules:
  0.0 25.0 jit_solution(14924283513251429368)
XLA Ops:
  1.3 22.5 %shard_map.85 = (f32[1,128]{1,0:T(1,128)S(1)}, bf16[1536,512]{1,0:T(8,128)(2,1)S(1)}, f32[192,128]{1,0:T(8,128)S(1)}) custom-call(s32[1,1,2,24]{3,2,1,0:T(2,128)} %bitcast.3, s32[1,1]{1,0:T(1,128)S(6)} %copy.9.cnt_hbm, bf16[128,5120]{1,0:T(8,128)(2,1)} %teacher_hbm.1, bf16[1,1,24,128,128]{4,3,2,1,0:T(8,128)(2,1)} %values_hbm.1, ...), custom_call_target="tpu_custom_call" | custom-call | tf_op jit(solution)/shard_map/pallas_call | solution.py:473
  23.8 1.2 %shard_map.86 = (f32[1,128]{1,0:T(1,128)}, bf16[1536,512]{1,0:T(8,128)(2,1)}, f32[192,128]{1,0:T(8,128)}) custom-call(f32[1,128]{1,0:T(1,128)S(1)} %get-tuple-element.9.div, bf16[1536,512]{1,0:T(8,128)(2,1)S(1)} %get-tuple-element.10.gw, f32[192,128]{1,0:T(8,128)S(1)} %get-tuple-element.11.gh), custom_call_target="tpu_custom_call" | custom-call | tf_op jit(solution)/shard_map/pallas_call | solution.py:516

commit v4 on v3

--- a/solution.py
+++ b/solution.py
@@ -174,12 +174,6 @@
             send_sem=pk_send, recv_sem=pk_recv.at[src],
             device_id={"tvoc": o}, device_id_type=MESH)
 
-    near = [k for k in range(1, n_t) if k % n_hi == 0 or k < n_hi]
-    away = [k for k in range(1, n_t) if k not in near]
-    for k in near:
-        packed_copy(spread(k), i).start()
-
-    pl.when(j != 0)(softmax)
     def to_all(ref, send, recv_near, recv_far):
         def start(ii, jj, recv):
             pltpu.make_async_remote_copy(
@@ -202,10 +196,20 @@
         lax.fori_loop(1, n_s, far, 0)
         lax.fori_loop(1, n_t, near, 0)
 
-    to_all(stats, st_send.at[0], st_recv.at[0], st_recv.at[1])
-    for k in away:
-        packed_copy(spread(k), i).start()
-
+    near = [k for k in range(1, n_t) if k % n_hi == 0 or k < n_hi]
+    away = [k for k in range(1, n_t) if k not in near]
+
+    def deliver(places):
+        for k in places:
+            packed_copy(spread(k), i).start()
+
+    def spread_early():
+        to_all(stats, st_send.at[0], st_recv.at[0], st_recv.at[1])
+
+    deliver(near)
+    pl.when(j != 0)(softmax)
+    spread_early()
+    deliver(away)
     def hidden_copy():
         start = pl.multiple_of(other * half, blk)
         return pltpu.make_async_remote_copy(
@@ -394,11 +398,26 @@
             jnp.sum(tm * logits[...], axis=1, keepdims=True)), 2)
         to_all(stats2, st_send.at[1], st_recv.at[2], st_recv.at[2])
 
-    turns = [*range(min(1, n_s - 2)), n_s - 2, *range(1, n_s - 2)]
-    for p in turns:
-        if p == n_s - 2:
-            pair_dots()
-        send_dots(p)
+    low = j // 2 * 2 < n_s // 2
+    others = list(range(n_s - 2))
+
+    def by_half(work):
+        kept = list(counts)
+        pl.when(low)(functools.partial(work, [n_s - 2, *others]))
+        counts[:] = kept
+        pl.when(jnp.logical_not(low))(functools.partial(work, [*others, n_s - 2]))
+
+    def send_all(turns):
+        for at, p in enumerate(turns):
+            send_dots(p)
+            if p == 0 or n_s == 2:
+                pair_dots()
+
+    def finish_all(turns):
+        for p in turns:
+            finish(p)
+
+    by_half(send_all)
     for p in range(n_s - 2):
         own[p] = chunk(i, order(p))
     own_mate[...] = chunk(i, mate, early)
@@ -407,8 +426,7 @@
     lg_copy.wait_recv()
     fill(tiles)
     own_send()
-    for p in turns:
-        finish(p)
+    by_half(finish_all)
     block_wait(stats2, n - 1, st_recv.at[2])
     late = jnp.sum(stats2[...], axis=0)
     entropy, cross = late[0:1], late[1:2]

time: 25.2 us -> 25 us (level)
  no operation moved by 1% of the time
where the time goes in v4:
time: 25 us; the launch traced here: 24.8 us
  Pallas kernels  23.5 us (94%)
  between operations  1.29 us (5%)
    pallas_call x1, Pallas kernels, local(): pl.pallas_call(functools.partial(kernel, n_t, n_s, blk), out_shape=(jax.S...  22.3 us
    pallas_call x1, Pallas kernels, local(): pl.pallas_call(flush, out_shape=tuple((jax.ShapeDtypeStruct(x.shape, x.dt...  1.19 us

profile of v4, /device:TPU:0, one launch (start us, length us, event | category | flops | bytes accessed | tf_op | source)
XLA Modules:
  0.0 24.8 jit_solution(7533605327383041139)
XLA Ops:
  1.3 22.3 %shard_map.85 = (f32[1,128]{1,0:T(1,128)S(1)}, bf16[1536,512]{1,0:T(8,128)(2,1)S(1)}, f32[192,128]{1,0:T(8,128)S(1)}) custom-call(s32[1,1,2,24]{3,2,1,0:T(2,128)} %bitcast.3, s32[1,1]{1,0:T(1,128)S(6)} %copy.9.cnt_hbm, bf16[128,5120]{1,0:T(8,128)(2,1)} %teacher_hbm.1, bf16[1,1,24,128,128]{4,3,2,1,0:T(8,128)(2,1)} %values_hbm.1, ...), custom_call_target="tpu_custom_call" | custom-call | tf_op jit(solution)/shard_map/pallas_call | solution.py:491
  23.6 1.2 %shard_map.86 = (f32[1,128]{1,0:T(1,128)}, bf16[1536,512]{1,0:T(8,128)(2,1)}, f32[192,128]{1,0:T(8,128)}) custom-call(f32[1,128]{1,0:T(1,128)S(1)} %get-tuple-element.9.div, bf16[1536,512]{1,0:T(8,128)(2,1)S(1)} %get-tuple-element.10.gw, f32[192,128]{1,0:T(8,128)S(1)} %get-tuple-element.11.gh), custom_call_target="tpu_custom_call" | custom-call | tf_op jit(solution)/shard_map/pallas_call | solution.py:534

commit v5 on v4

--- a/solution.py
+++ b/solution.py
@@ -487,7 +487,7 @@
         V((n_t, early, tokens), bf16),
         V((rest, tokens), bf16),
     ]
-    parts = 3 if width % (3 * 128) == 0 else 1
+    parts = 6 if width % (6 * 128) == 0 else 1
     div, gw, gh = pl.pallas_call(
         functools.partial(kernel, n_t, n_s, blk),
         out_shape=(

time: 25 us -> 25.1 us (level)
  no operation moved by 1% of the time
where the time goes in v5:
time: 25.1 us; the launch traced here: 24.9 us
  Pallas kernels  23.7 us (94%)
  between operations  1.29 us (5%)
    pallas_call x1, Pallas kernels, local(): pl.pallas_call(functools.partial(kernel, n_t, n_s, blk), out_shape=(jax.S...  22.5 us
    pallas_call x1, Pallas kernels, local(): pl.pallas_call(flush, out_shape=tuple((jax.ShapeDtypeStruct(x.shape, x.dt...  1.19 us

profile of v5, /device:TPU:0, one launch (start us, length us, event | category | flops | bytes accessed | tf_op | source)
XLA Modules:
  0.0 24.9 jit_solution(2277447346140070129)
XLA Ops:
  1.3 22.5 %shard_map.85 = (f32[1,128]{1,0:T(1,128)S(1)}, bf16[1536,512]{1,0:T(8,128)(2,1)S(1)}, f32[192,128]{1,0:T(8,128)S(1)}) custom-call(s32[1,1,2,24]{3,2,1,0:T(2,128)} %bitcast.3, s32[1,1]{1,0:T(1,128)S(6)} %copy.9.cnt_hbm, bf16[128,5120]{1,0:T(8,128)(2,1)} %teacher_hbm.1, bf16[1,1,24,128,128]{4,3,2,1,0:T(8,128)(2,1)} %values_hbm.1, ...), custom_call_target="tpu_custom_call" | custom-call | tf_op jit(solution)/shard_map/pallas_call | solution.py:491
  23.7 1.2 %shard_map.86 = (f32[1,128]{1,0:T(1,128)}, bf16[1536,512]{1,0:T(8,128)(2,1)}, f32[192,128]{1,0:T(8,128)}) custom-call(f32[1,128]{1,0:T(1,128)S(1)} %get-tuple-element.9.div, bf16[1536,512]{1,0:T(8,128)(2,1)S(1)} %get-tuple-element.10.gw, f32[192,128]{1,0:T(8,128)S(1)} %get-tuple-element.11.gh), custom_call_target="tpu_custom_call" | custom-call | tf_op jit(solution)/shard_map/pallas_call | solution.py:534
